TPU v7x, 32 devices: a whole 2x2x4 slice. The times are simulated.
32 devices in a mesh: tm: 2 (over x), chan: 4 (over y, core), bl: 4 (over z).
Axes of the slice: x: 2, y: 2, z: 4, core: 2. Of those that a mesh axis runs over, the one named last changes fastest.
Arguments:
- voltages: bfloat16 [2, 256, 128, 512], P(None, ('chan', 'bl'), None, 'tm'), may hold values from -6 to 6
Outputs:
- visibilities: bfloat16 [2, 128, 4, 256, 256], P(None, ('chan', 'bl'), 'tm')
All inputs are finite; a program needn't handle non-finite values.
Results may differ from a plain program's by a relative error of at most 0.0051.
Values may be sent and summed in bfloat16 or wider, within the bound.
A program may use at most 64 MiB of HBM per device.

v0:
```python
import jax
import jax.numpy as jnp
from jax import lax
from jax.sharding import PartitionSpec as P

HALF = 128


def passed_along(block, axis, distance):
    devices = range(lax.axis_size(axis))
    route = [(i - distance, i) for i in devices if i - distance in devices]
    return lax.ppermute(block, axis, route)


def tapers(length):
    steps = jnp.arange(length, dtype=jnp.float32)
    taper_early = jnp.sin(jnp.pi * (steps + 0.5) / (2.0 * length))
    taper_late = jnp.sin(jnp.pi * (steps + 0.5 + length) / (2.0 * length))
    return (taper_early, taper_late)


def weighted(block, taper):
    return (block.astype(jnp.float32) * taper).astype(jnp.bfloat16)


def products(stacked):
    signals = stacked.shape[0] // 2
    gram = jnp.einsum("pct,qct->cpq", stacked, stacked, preferred_element_type=jnp.float32)
    real_part = gram[:, :signals, :signals] + gram[:, signals:, signals:]
    imag_part = gram[:, signals:, :signals] - gram[:, :signals, signals:]
    return (real_part, imag_part)


def local(voltages):
    turned = lax.all_to_all(voltages, ("chan", "bl"), split_axis=2, concat_axis=1, tiled=True)
    signals = turned.shape[1]
    channels = turned.shape[2]
    samples = turned.shape[3]
    halves = samples // HALF
    scale = 1.0 / HALF
    taper_early, taper_late = tapers(HALF)
    stacked = turned.reshape(2 * signals, channels, samples)
    lates = []
    earlies = []
    for index in range(halves):
        piece = stacked[:, :, index * HALF : (index + 1) * HALF]
        lates.append(products(weighted(piece, taper_late)))
        if index + 1 < halves:
            earlies.append(products(weighted(piece, taper_early)))
    tail = turned[:, :, :, samples - HALF :]
    received = passed_along(tail, "tm", 1)
    previous = products(weighted(received.reshape(2 * signals, channels, HALF), taper_early))
    real_list = []
    imag_list = []
    for index in range(halves):
        late_real, late_imag = lates[index]
        real_list.append(((late_real + previous[0]) * scale).astype(jnp.bfloat16))
        imag_list.append(((late_imag + previous[1]) * scale).astype(jnp.bfloat16))
        if index + 1 < halves:
            previous = earlies[index]
    return jnp.stack([jnp.stack(real_list, 1), jnp.stack(imag_list, 1)], 0)


def solution(mesh):
    return jax.shard_map(
        local,
        mesh=mesh,
        in_specs=(P(None, ("chan", "bl"), None, "tm"),),
        out_specs=P(None, ("chan", "bl"), "tm", None, None),
        check_vma=False,
    )
```

profile of v0, /device:TPU:0, one launch (start us, length us, event | category | flops | bytes accessed | tf_op | source)
XLA Modules:
  0.0 100.2 jit_solution(14008793336782749242)
XLA Ops:
  0.0 2.8 %copy.22 = bf16[2,16,128,256]{3,1,0,2:T(8,128)(2,1)S(1)} copy(bf16[2,16,128,256]{3,2,1,0:T(8,128)(2,1)} %param.1) | data formatting | bytes 4194304 | tf_op args[0]
  2.8 56.5 %all_to_all.18 = bf16[2,16,128,256]{3,1,0,2:T(8,128)(2,1)S(1)} all-to-all(bf16[2,16,128,256]{3,1,0,2:T(8,128)(2,1)S(1)} %copy.22), channel_id=1, replica_groups=mesh['tm'=2,'chan'=4,'bl'=4] {'chan','bl'}, dimensions={2} | all-to-all | bytes 4194304 | tf_op jit(solution)/shard_map/all_to_all | solution.py:35
  59.3 1.7 %copy.24 = bf16[2,16,16,8,256]{4,3,2,1,0:T(8,128)(2,1)S(1)} copy(bf16[2,16,16,8,256]{4,2,0,3,1:T(8,128)(2,1)S(1)} %bitcast.24) | data formatting | bytes 4194304 | tf_op jit(solution)/shard_map/all_to_all | solution.py:35
  61.0 0.1 slice.79
  61.1 3.6 %collective-permute-start = (bf16[2,256,8,128]{3,2,1,0:T(8,128)(2,1)S(1)}, bf16[2,256,8,128]{3,2,1,0:T(8,128)(2,1)S(1)}, u32[]{:S(2)}, u32[]{:S(2)}) collective-permute-start(bf16[2,256,8,128]{3,2,1,0:T(8,128)(2,1)S(1)} %slice.79), channel_id=1, source_target_pairs={{0,16},{1,17},{2,18},{3,19},{4,20},{5,21},{6,22},{7,23},{8,24},{9,... | collective-permute-start | bytes 3145736 | tf_op jit(solution)/shard_map/ppermute | solution.py:12
  64.7 0.1 multiply_sine_fusion
  64.8 22.0 %collective-permute-done = bf16[2,256,8,128]{3,2,1,0:T(8,128)(2,1)S(1)} collective-permute-done((bf16[2,256,8,128]{3,2,1,0:T(8,128)(2,1)S(1)}, bf16[2,256,8,128]{3,2,1,0:T(8,128)(2,1)S(1)}, u32[]{:S(2)}, u32[]{:S(2)}) %collective-permute-start) | collective-permute-done | bytes 1048608 | tf_op jit(solution)/shard_map/ppermute | solution.py:12
  86.8 0.8 fusion
  87.7 1.3 %fusion.23 = f32[8,512,512]{2,1,0:T(8,128)S(1)} fusion(bf16[512,8,128]{2,1,0:T(8,128)(2,1)S(1)} %get-tuple-element.12), kind=kOutput, calls=%fused_computation.38 | convolution fusion | flops 536870912 | bytes 9437184 | tf_op jit(solution)/shard_map/pct,qct->cpq/dot_general | solution.py:28
  88.9 1.3 %fusion.25 = f32[8,512,512]{2,1,0:T(8,128)S(1)} fusion(bf16[512,8,128]{2,1,0:T(8,128)(2,1)S(1)} %get-tuple-element.9), kind=kOutput, calls=%fused_computation.40 | convolution fusion | flops 536870912 | bytes 9437184 | tf_op jit(solution)/shard_map/pct,qct->cpq/dot_general | solution.py:28
  90.2 1.3 %fusion.19 = f32[8,512,512]{2,1,0:T(8,128)S(1)} fusion(bf16[512,8,128]{2,1,0:T(8,128)(2,1)S(1)} %get-tuple-element.11), kind=kOutput, calls=%fused_computation.34 | convolution fusion | flops 536870912 | bytes 9437184 | tf_op jit(solution)/shard_map/pct,qct->cpq/dot_general | solution.py:28
  91.5 1.3 %fusion.21 = f32[8,512,512]{2,1,0:T(8,128)S(1)} fusion(bf16[512,8,128]{2,1,0:T(8,128)(2,1)S(1)} %get-tuple-element.10), kind=kOutput, calls=%fused_computation.36 | convolution fusion | flops 536870912 | bytes 9437184 | tf_op jit(solution)/shard_map/pct,qct->cpq/dot_general | solution.py:28
  92.7 2.2 %fusion.15 = (bf16[8,1,256,256]{3,2,0,1:T(8,128)(2,1)S(1)}, bf16[8,1,256,256]{3,2,0,1:T(8,128)(2,1)S(1)}) fusion(f32[8,512,512]{2,1,0:T(8,128)S(1)} %fusion.23, f32[8,512,512]{2,1,0:T(8,128)S(1)} %fusion.25), kind=kLoop, calls=%fused_computation.30 | loop fusion | flops 5242880 | bytes 18874368 | tf_op jit(solution)/shard_map/stack | solution.py:61
  94.9 2.2 %fusion.16 = (bf16[8,1,256,256]{3,2,0,1:T(8,128)(2,1)S(1)}, bf16[8,1,256,256]{3,2,0,1:T(8,128)(2,1)S(1)}) fusion(f32[8,512,512]{2,1,0:T(8,128)S(1)} %fusion.19, f32[8,512,512]{2,1,0:T(8,128)S(1)} %fusion.21), kind=kLoop, calls=%fused_computation.31 | loop fusion | flops 5242880 | bytes 18874368 | tf_op jit(solution)/shard_map/stack | solution.py:61
  97.2 0.2 maximum_bitcast_fusion
  97.4 0.2 maximum_bitcast_fusion.1
  97.6 0.4 pad_maximum_fusion
  98.0 2.3 %copy.34 = bf16[2,8,2,256,256]{4,3,2,1,0:T(8,128)(2,1)} copy(bf16[2,8,2,256,256]{4,3,1,2,0:T(8,128)(2,1)S(1)} %pad_maximum_fusion) | data formatting | bytes 8388608 | tf_op jit(solution)/shard_map/stack | solution.py:61
Async XLA Ops:
  61.1 25.8 %collective-permute-start = (bf16[2,256,8,128]{3,2,1,0:T(8,128)(2,1)S(1)}, bf16[2,256,8,128]{3,2,1,0:T(8,128)(2,1)S(1)}, u32[]{:S(2)}, u32[]{:S(2)}) collective-permute-start(bf16[2,256,8,128]{3,2,1,0:T(8,128)(2,1)S(1)} %slice.79), channel_id=1, source_target_pairs={{0,16},{1,17},{2,18},{3,19},{4,20},{5,21},{6,22},{7,23},{8,24},{9,... | collective-permute-start | bytes 3145736 | tf_op jit(solution)/shard_map/ppermute | solution.py:12
where the time goes:
time: 100 us
  blocking collectives  56.5 us (56%)
  waiting for transfers between devices  22 us (22%)
  local copies, waits for them, and re-layouts  6.84 us (7%)
  other arithmetic  6.05 us (6%)
  matrix products  5.05 us (5%)
  starting transfers between devices  3.64 us (4%)
    all_to_all x1, blocking collectives, local(): lax.all_to_all(voltages, ('chan', 'bl'), split_axis=2, concat_axis=1, til...  56.5 us
    ppermute x1, waiting for transfers between devices, passed_along(): return lax.ppermute(block, axis, route)  22 us
    another operation x5, other arithmetic, local(): return jnp.stack([jnp.stack(real_list, 1), jnp.stack(imag_list, 1)], 0)  5.19 us
    dot_general x4, matrix products, products(): jnp.einsum('pct,qct->cpq', stacked, stacked, preferred_element_type=jnp.f...  5.05 us
    ppermute x1, starting transfers between devices, passed_along(): return lax.ppermute(block, axis, route)  3.64 us
    unnamed x1, local copies, waits for them, and re-layouts  2.76 us
    another operation x1, local copies, waits for them, and re-layouts, local(): return jnp.stack([jnp.stack(real_list, 1), jnp.stack(imag_list, 1)], 0)  2.29 us
  transfers between devices with their start and end apart: 1, of which 1 were waited for; matrix products, arithmetic and copies ran while one was open for 0% of the time, Pallas kernels for 0%

commit v1 on v0

--- a/solution.py
+++ b/solution.py
@@ -32,7 +32,15 @@
 
 
 def local(voltages):
-    turned = lax.all_to_all(voltages, ("chan", "bl"), split_axis=2, concat_axis=1, tiled=True)
+    turned = jnp.concatenate(
+        lax.all_to_all(
+            jnp.stack(jnp.split(voltages, lax.axis_size(("chan", "bl")), axis=2)),
+            ("chan", "bl"),
+            0,
+            0,
+        ),
+        axis=1,
+    )
     signals = turned.shape[1]
     channels = turned.shape[2]
     samples = turned.shape[3]

time: 100 us -> 111 us (1.11)
  local copies, waits for them, and re-layouts: 6.84 us -> 17.2 us
    unnamed x1 -> x15, local copies, waits for them, and re-layouts: 2.76 us -> 13.8 us
    all_to_all x1, local copies, waits for them, and re-layouts: 1.72 us -> 0.14 us  [local(): lax.all_to_all(jnp.stack(jnp.split(voltages, lax.axis_size(('chan', 'bl')...]
where the time goes in v1:
time: 111 us
  blocking collectives  56.5 us (51%)
  waiting for transfers between devices  22.2 us (20%)
  local copies, waits for them, and re-layouts  17.2 us (15%)
  other arithmetic  6.05 us (5%)
  matrix products  5.05 us (5%)
  starting transfers between devices  3.46 us (3%)
    all_to_all x1, blocking collectives, local(): lax.all_to_all(jnp.stack(jnp.split(voltages, lax.axis_size(('chan', 'bl')...  56.5 us
    ppermute x1, waiting for transfers between devices, passed_along(): return lax.ppermute(block, axis, route)  22.2 us
    unnamed x15, local copies, waits for them, and re-layouts  13.8 us
    another operation x5, other arithmetic, local(): return jnp.stack([jnp.stack(real_list, 1), jnp.stack(imag_list, 1)], 0)  5.19 us
    dot_general x4, matrix products, products(): jnp.einsum('pct,qct->cpq', stacked, stacked, preferred_element_type=jnp.f...  5.05 us
    ppermute x1, starting transfers between devices, passed_along(): return lax.ppermute(block, axis, route)  3.46 us
    another operation x1, local copies, waits for them, and re-layouts, local(): return jnp.stack([jnp.stack(real_list, 1), jnp.stack(imag_list, 1)], 0)  2.29 us
  transfers between devices with their start and end apart: 1, of which 1 were waited for; matrix products, arithmetic and copies ran while one was open for 0% of the time, Pallas kernels for 0%

profile of v1, /device:TPU:0, one launch (start us, length us, event | category | flops | bytes accessed | tf_op | source)
XLA Modules:
  0.0 110.6 jit_solution(12216870350781147445)
XLA Ops:
  0.0 0.9 bitcast_dynamic-update-slice_fusion.15
  0.9 0.9 bitcast_dynamic-update-slice_fusion.14
  1.8 0.9 bitcast_dynamic-update-slice_fusion.13
  2.8 0.9 bitcast_dynamic-update-slice_fusion.12
  3.7 0.9 bitcast_dynamic-update-slice_fusion.11
  4.6 0.9 bitcast_dynamic-update-slice_fusion.10
  5.5 0.9 bitcast_dynamic-update-slice_fusion.9
  6.4 0.9 bitcast_dynamic-update-slice_fusion.8
  7.4 0.9 bitcast_dynamic-update-slice_fusion.7
  8.3 0.9 bitcast_dynamic-update-slice_fusion.6
  9.2 0.9 bitcast_dynamic-update-slice_fusion.5
  10.1 0.9 bitcast_dynamic-update-slice_fusion.4
  11.0 0.9 bitcast_dynamic-update-slice_fusion.3
  12.0 0.9 bitcast_dynamic-update-slice_fusion.2
  12.9 0.9 bitcast_dynamic-update-slice_fusion.1
  13.8 0.9 bitcast_dynamic-update-slice_fusion
  14.7 56.5 %all_to_all.5 = bf16[16,2,16,8,256]{4,3,2,1,0:T(8,128)(2,1)S(1)} all-to-all(bf16[16,2,16,8,256]{4,3,2,1,0:T(8,128)(2,1)S(1)} %bitcast_dynamic-update-slice_fusion), channel_id=1, replica_groups=mesh['tm'=2,'chan'=4,'bl'=4] {'chan','bl'}, dimensions={0} | all-to-all | bytes 4194304 | tf_op jit(solution)/shard_map/all_to_all | solution.py:36
  71.2 0.1 copy.12
  71.4 0.1 slice.79
  71.5 3.5 %collective-permute-start = (bf16[2,256,8,128]{3,2,1,0:T(8,128)(2,1)S(1)}, bf16[2,256,8,128]{3,2,1,0:T(8,128)(2,1)S(1)}, u32[]{:S(2)}, u32[]{:S(2)}) collective-permute-start(bf16[2,256,8,128]{3,2,1,0:T(8,128)(2,1)S(1)} %slice.79), channel_id=1, source_target_pairs={{0,16},{1,17},{2,18},{3,19},{4,20},{5,21},{6,22},{7,23},{8,24},{9,... | collective-permute-start | bytes 3145736 | tf_op jit(solution)/shard_map/ppermute | solution.py:12
  74.9 0.1 multiply_sine_fusion
  75.0 22.2 %collective-permute-done = bf16[2,256,8,128]{3,2,1,0:T(8,128)(2,1)S(1)} collective-permute-done((bf16[2,256,8,128]{3,2,1,0:T(8,128)(2,1)S(1)}, bf16[2,256,8,128]{3,2,1,0:T(8,128)(2,1)S(1)}, u32[]{:S(2)}, u32[]{:S(2)}) %collective-permute-start) | collective-permute-done | bytes 1048608 | tf_op jit(solution)/shard_map/ppermute | solution.py:12
  97.2 0.8 fusion
  98.0 1.3 %fusion.23 = f32[8,512,512]{2,1,0:T(8,128)S(1)} fusion(bf16[512,8,128]{2,1,0:T(8,128)(2,1)S(1)} %get-tuple-element.12), kind=kOutput, calls=%fused_computation.38 | convolution fusion | flops 536870912 | bytes 9437184 | tf_op jit(solution)/shard_map/pct,qct->cpq/dot_general | solution.py:28
  99.3 1.3 %fusion.25 = f32[8,512,512]{2,1,0:T(8,128)S(1)} fusion(bf16[512,8,128]{2,1,0:T(8,128)(2,1)S(1)} %get-tuple-element.9), kind=kOutput, calls=%fused_computation.40 | convolution fusion | flops 536870912 | bytes 9437184 | tf_op jit(solution)/shard_map/pct,qct->cpq/dot_general | solution.py:28
  100.6 1.3 %fusion.19 = f32[8,512,512]{2,1,0:T(8,128)S(1)} fusion(bf16[512,8,128]{2,1,0:T(8,128)(2,1)S(1)} %get-tuple-element.11), kind=kOutput, calls=%fused_computation.34 | convolution fusion | flops 536870912 | bytes 9437184 | tf_op jit(solution)/shard_map/pct,qct->cpq/dot_general | solution.py:28
  101.8 1.3 %fusion.21 = f32[8,512,512]{2,1,0:T(8,128)S(1)} fusion(bf16[512,8,128]{2,1,0:T(8,128)(2,1)S(1)} %get-tuple-element.10), kind=kOutput, calls=%fused_computation.36 | convolution fusion | flops 536870912 | bytes 9437184 | tf_op jit(solution)/shard_map/pct,qct->cpq/dot_general | solution.py:28
  103.1 2.2 %fusion.15 = (bf16[8,1,256,256]{3,2,0,1:T(8,128)(2,1)S(1)}, bf16[8,1,256,256]{3,2,0,1:T(8,128)(2,1)S(1)}) fusion(f32[8,512,512]{2,1,0:T(8,128)S(1)} %fusion.23, f32[8,512,512]{2,1,0:T(8,128)S(1)} %fusion.25), kind=kLoop, calls=%fused_computation.30 | loop fusion | flops 5242880 | bytes 18874368 | tf_op jit(solution)/shard_map/stack | solution.py:69
  105.3 2.2 %fusion.16 = (bf16[8,1,256,256]{3,2,0,1:T(8,128)(2,1)S(1)}, bf16[8,1,256,256]{3,2,0,1:T(8,128)(2,1)S(1)}) fusion(f32[8,512,512]{2,1,0:T(8,128)S(1)} %fusion.19, f32[8,512,512]{2,1,0:T(8,128)S(1)} %fusion.21), kind=kLoop, calls=%fused_computation.31 | loop fusion | flops 5242880 | bytes 18874368 | tf_op jit(solution)/shard_map/stack | solution.py:69
  107.5 0.2 maximum_bitcast_fusion
  107.7 0.2 maximum_bitcast_fusion.1
  107.9 0.4 pad_maximum_fusion
  108.3 2.3 %copy.21 = bf16[2,8,2,256,256]{4,3,2,1,0:T(8,128)(2,1)} copy(bf16[2,8,2,256,256]{4,3,1,2,0:T(8,128)(2,1)S(1)} %pad_maximum_fusion) | data formatting | bytes 8388608 | tf_op jit(solution)/shard_map/stack | solution.py:69
Async XLA Ops:
  71.5 25.8 %collective-permute-start = (bf16[2,256,8,128]{3,2,1,0:T(8,128)(2,1)S(1)}, bf16[2,256,8,128]{3,2,1,0:T(8,128)(2,1)S(1)}, u32[]{:S(2)}, u32[]{:S(2)}) collective-permute-start(bf16[2,256,8,128]{3,2,1,0:T(8,128)(2,1)S(1)} %slice.79), channel_id=1, source_target_pairs={{0,16},{1,17},{2,18},{3,19},{4,20},{5,21},{6,22},{7,23},{8,24},{9,... | collective-permute-start | bytes 3145736 | tf_op jit(solution)/shard_map/ppermute | solution.py:12
